TPU v7x, 32 devices: a whole 2x2x4 slice. The times are simulated.
32 devices in a mesh: dp: 4 (over y, x), shard: 8 (over z, core).
Axes of the slice: x: 2, y: 2, z: 4, core: 2. Of those that a mesh axis runs over, the one named last changes fastest.
Arguments:
- gradients: bfloat16 [4, 4, 786432], P('dp', None, 'shard'), may hold values from -32 to 32
- master: float32 [3145728], P(('dp', 'shard'))
- moment: float32 [3145728], P(('dp', 'shard')), may hold values from -1.5 to 1.5
- second: float32 [3145728], P(('dp', 'shard')), may hold values from 0.05 to 2
- segment_ids: int32 [24576], P(('dp', 'shard')), may hold values from 0 to 15, never falling along the last dimension, each value on 1 to 3072 neighbouring positions
Outputs:
- weights: bfloat16 [4, 786432], P(None, 'shard')
- new_master: float32 [3145728], P(('dp', 'shard'))
- new_moment: float32 [3145728], P(('dp', 'shard'))
- new_second: float32 [3145728], P(('dp', 'shard'))
Inputs may be any that keep to these rules, and one draw needn't show every extreme that they name: segment_ids never falls along the flat vector; each tensor has 1 to 3072 blocks and one has exactly 3072.
All inputs are finite; a program needn't handle non-finite values.
Results may differ from a plain program's by a relative error of at most 0.0004.
Values may be sent and summed in bfloat16 or wider, within the bound.
No kernel may reach another device: no remote copies, remote signals or barrier semaphores. Data moves between devices by JAX's collectives and lax.ppermute only.
A program may use at most 64 MiB of HBM per device.

v0:
```python
import jax
import jax.numpy as jnp
from jax import lax
from jax.sharding import PartitionSpec as P

first_fix = 1.0 - 0.9**20
second_fix = 1.0 - 0.999**20
learn_rate = 0.2
decay_rate = 0.01
tiny_eps = 1e-06


def moments(summed, master_part, moment_part, second_part, replicas):
    grad = summed / replicas
    next_moment = 0.9 * moment_part + 0.1 * grad
    next_second = 0.999 * second_part + 0.001 * grad * grad
    update_dir = (
        next_moment / first_fix / (jnp.sqrt(next_second / second_fix) + tiny_eps)
        + decay_rate * master_part
    )
    return (next_moment, next_second, update_dir)


def tensor_sums(values, onehot):
    block_sq = jnp.sum((values * values).reshape(onehot.shape[0], -1), axis=1)
    return jnp.dot(block_sq, onehot, precision=lax.Precision.HIGHEST)


def on_device(gradients, master, moment, second, segment_ids):
    replicas = lax.axis_size("dp")
    tensors = lax.axis_size("dp") * lax.axis_size("shard") // 2
    blocks = segment_ids.shape[0]
    onehot = (segment_ids[:, None] == jnp.arange(tensors, dtype=jnp.int32)[None, :]).astype(
        jnp.float32
    )
    received = lax.all_to_all(gradients[0], "dp", split_axis=0, concat_axis=0, tiled=True)
    summed = jnp.sum(received.astype(jnp.float32), axis=0)
    new_moment, new_second, update_dir = moments(summed, master, moment, second, replicas)
    weight_sq, update_sq = lax.psum(
        (tensor_sums(master, onehot), tensor_sums(update_dir, onehot)), ("dp", "shard")
    )
    trust = jnp.sqrt(weight_sq) / (jnp.sqrt(update_sq) + tiny_eps)
    block_trust = jnp.dot(onehot, trust, precision=lax.Precision.HIGHEST)
    new_master = master - learn_rate * (
        update_dir.reshape(blocks, -1) * block_trust[:, None]
    ).reshape(-1)
    rounded = new_master.astype(jnp.bfloat16)[None, :]
    weights = lax.all_gather(rounded, "dp", axis=0, tiled=True)
    return (weights, new_master, new_moment, new_second)


def solution(mesh):
    placed = (
        P("dp", None, "shard"),
        P(("dp", "shard")),
        P(("dp", "shard")),
        P(("dp", "shard")),
        P(("dp", "shard")),
    )
    return jax.shard_map(
        on_device,
        mesh=mesh,
        in_specs=placed,
        out_specs=(P(None, "shard"), P(("dp", "shard")), P(("dp", "shard")), P(("dp", "shard"))),
        check_vma=False,
    )
```

profile of v0, /device:TPU:0, one launch (start us, length us, event | category | flops | bytes accessed | tf_op | source)
XLA Modules:
  0.0 80.3 jit_solution(6110811445067844543)
XLA Ops:
  0.6 0.5 broadcast.17
  1.1 2.8 %reduce.3 = bf16[4,98304]{1,0:T(4,128)(2,1)S(1)} reduce(bf16[4,1,98304]{2,0,1:T(4,128)(2,1)} %bitcast.21, bf16[]{:T(256)} %broadcast.17), dimensions={1}, to_apply=%copy.10.reduce_sub_computation | reduce | bytes 1572866 | tf_op jit(solution)/shard_map/all_to_all | solution.py:36
  3.9 0.8 reshape.33
  4.7 16.3 %all_to_all.9 = bf16[4,2,49152]{2,1,0:T(2,128)(2,1)S(1)} all-to-all(bf16[4,2,49152]{2,1,0:T(2,128)(2,1)S(1)} %reshape.33), channel_id=1, replica_groups=mesh['dp'=4,'shard'=8] {'dp'}, dimensions={0} | all-to-all | bytes 1572864 | tf_op jit(solution)/shard_map/all_to_all | solution.py:36
  21.0 0.0 copy-start
  21.0 0.7 reshape.34
  21.8 2.4 %convert_reduce_fusion = f32[98304]{0:T(1024)S(1)} fusion(bf16[4,1,98304]{2,1,0:T(2,128)(2,1)S(1)} %reshape.34), kind=kLoop, calls=%fused_computation | loop fusion | flops 688128 | bytes 1179648 | tf_op jit(solution)/shard_map/reduce_sum | solution.py:37
  24.2 0.0 copy-done
  24.2 0.0 copy-done.3
  24.2 0.0 copy-done.4
  24.2 0.0 copy-start.5
  24.3 0.4 bitcast_reduce_fusion.1
  24.7 0.0 copy-start.1
  24.7 0.0 copy-start.2
  24.7 0.2 copy-done.5
  24.9 0.3 convolution_bitcast_fusion.1
  25.3 0.3 convolution_bitcast_fusion
  25.6 39.5 %all-reduce = (f32[16]{0:T(128)S(1)}, f32[16]{0:T(128)S(1)}) all-reduce(f32[16]{0:T(128)S(1)} %convolution_bitcast_fusion, f32[16]{0:T(128)S(1)} %convolution_bitcast_fusion.1), channel_id=1, replica_groups=mesh['dp'=4,'shard'=8] {'dp','shard'}, use_global_device_ids=true, to_apply=%region_4.0 | all-reduce | flops 32 | bytes 256 | tf_op jit(solution)/shard_map/psum | solution.py:39
  65.1 0.4 convolution_reduce_fusion
  65.5 1.0 %fusion.10 = (bf16[98304]{0:T(1024)(128)(2,1)S(1)}, f32[98304]{0:T(1024)}) fusion(f32[98304]{0:T(1024)S(1)} %copy-done, f32[768]{0:T(1024)S(1)} %convolution_reduce_fusion, f32[98304]{0:T(1024)S(1)} %get-tuple-element.11, f32[98304]{0:T(1024)S(1)} %get-tuple-element.10), kind=kLoop, calls=%fused_computation.22 | loop fusion | flops 983040 | bytes 1772544 | tf_op jit(solution)/shard_map/convert_element_type | solution.py:47
  66.5 12.6 %all-gather = bf16[393216]{0:T(1024)(128)(2,1)S(1)} all-gather(bf16[98304]{0:T(1024)(128)(2,1)S(1)} %get-tuple-element.8), channel_id=2, replica_groups=mesh['dp'=4,'shard'=8] {'dp'}, dimensions={0}, use_global_device_ids=true | all-gather | bytes 983040 | tf_op jit(solution)/shard_map/all_gather | solution.py:48
  79.1 1.2 %reshape.25 = bf16[4,98304]{1,0:T(4,128)(2,1)} reshape(bf16[393216]{0:T(1024)(128)(2,1)S(1)} %all-gather) | data formatting | bytes 1572864 | tf_op jit(solution)/shard_map/all_gather | solution.py:48
  80.3 0.0 copy-done.1
  80.3 0.0 copy-done.2
  (4 shorter events, 0.0 us)
Async XLA Ops:
  21.0 3.2 %copy-start = (f32[98304]{0:T(1024)S(1)}, f32[98304]{0:T(1024)}, u32[]{:S(2)}) copy-start(f32[98304]{0:T(1024)} %param.6) | copy-start | bytes 1179652
  21.0 3.2 %copy-start.3 = (f32[98304]{0:T(1024)S(1)}, f32[98304]{0:T(1024)}, u32[]{:S(2)}) copy-start(f32[98304]{0:T(1024)} %param.7) | copy-start | bytes 1179652
  21.0 3.2 %copy-start.4 = (f32[98304]{0:T(1024)S(1)}, f32[98304]{0:T(1024)}, u32[]{:S(2)}) copy-start(f32[98304]{0:T(1024)} %param.8) | copy-start | bytes 1179652
  24.2 0.7 copy-start.5
  24.7 55.6 %copy-start.1 = (f32[98304]{0:T(1024)}, f32[98304]{0:T(1024)S(1)}, u32[]{:S(2)}) copy-start(f32[98304]{0:T(1024)S(1)} %get-tuple-element.10) | copy-start | bytes 1179652
  24.7 55.6 %copy-start.2 = (f32[98304]{0:T(1024)}, f32[98304]{0:T(1024)S(1)}, u32[]{:S(2)}) copy-start(f32[98304]{0:T(1024)S(1)} %get-tuple-element.11) | copy-start | bytes 1179652
where the time goes:
time: 80.6 us; the launch traced here: 80.3 us
  blocking collectives  68.4 us (85%)
  other arithmetic  6.61 us (8%)
  local copies, waits for them, and re-layouts  3.45 us (4%)
  matrix products  1.05 us (1%)
    psum x1, blocking collectives, on_device(): lax.psum((tensor_sums(master, onehot), tensor_sums(update_dir, onehot)),...  39.5 us
    all_to_all x1, blocking collectives, on_device(): lax.all_to_all(gradients[0], 'dp', split_axis=0, concat_axis=0, tiled=True)  16.3 us
    all_gather x1, blocking collectives, on_device(): weights = lax.all_gather(rounded, 'dp', axis=0, tiled=True)  12.6 us
    all_to_all x1, other arithmetic, on_device(): lax.all_to_all(gradients[0], 'dp', split_axis=0, concat_axis=0, tiled=True)  2.75 us
    reduce_sum x1, other arithmetic, on_device(): summed = jnp.sum(received.astype(jnp.float32), axis=0)  2.43 us
    unnamed x14, local copies, waits for them, and re-layouts  1.76 us

commit v1 on v0

--- a/solution.py
+++ b/solution.py
@@ -37,7 +37,7 @@
     summed = jnp.sum(received.astype(jnp.float32), axis=0)
     new_moment, new_second, update_dir = moments(summed, master, moment, second, replicas)
     weight_sq, update_sq = lax.psum(
-        (tensor_sums(master, onehot), tensor_sums(update_dir, onehot)), ("dp", "shard")
+        lax.psum((tensor_sums(master, onehot), tensor_sums(update_dir, onehot)), "shard"), "dp"
     )
     trust = jnp.sqrt(weight_sq) / (jnp.sqrt(update_sq) + tiny_eps)
     block_trust = jnp.dot(onehot, trust, precision=lax.Precision.HIGHEST)

time: 80.6 us -> 63.4 us (0.79)
  blocking collectives: 68.4 us -> 51.2 us
    psum x1, blocking collectives: 39.5 us -> 15.1 us  [on_device(): lax.psum((tensor_sums(master, onehot), tensor_sums(update_dir, onehot)),...]
    psum x0 -> x1, blocking collectives: none -> 8.72 us  [on_device(): lax.psum(lax.psum((tensor_sums(master, onehot), tensor_sums(update_dir, o...]
    all_gather x1, blocking collectives: 12.6 us -> 11 us  [on_device(): weights = lax.all_gather(rounded, 'dp', axis=0, tiled=True)]
where the time goes in v1:
time: 63.4 us; the launch traced here: 63.1 us
  blocking collectives  51.2 us (81%)
  other arithmetic  6.61 us (10%)
  local copies, waits for them, and re-layouts  3.45 us (5%)
  matrix products  1.06 us (2%)
  between operations  0.75 us (1%)
    all_to_all x1, blocking collectives, on_device(): lax.all_to_all(gradients[0], 'dp', split_axis=0, concat_axis=0, tiled=True)  16.3 us
    psum x1, blocking collectives, on_device(): lax.psum((tensor_sums(master, onehot), tensor_sums(update_dir, onehot)),...  15.1 us
    all_gather x1, blocking collectives, on_device(): weights = lax.all_gather(rounded, 'dp', axis=0, tiled=True)  11 us
    psum x1, blocking collectives, on_device(): lax.psum(lax.psum((tensor_sums(master, onehot), tensor_sums(update_dir, o...  8.72 us
    all_to_all x1, other arithmetic, on_device(): lax.all_to_all(gradients[0], 'dp', split_axis=0, concat_axis=0, tiled=True)  2.75 us
    reduce_sum x1, other arithmetic, on_device(): summed = jnp.sum(received.astype(jnp.float32), axis=0)  2.43 us
    unnamed x14, local copies, waits for them, and re-layouts  1.76 us

profile of v1, /device:TPU:0, one launch (start us, length us, event | category | flops | bytes accessed | tf_op | source)
XLA Modules:
  0.0 63.1 jit_solution(11203071899683855664)
XLA Ops:
  0.6 0.5 broadcast.17
  1.1 2.8 %reduce.3 = bf16[4,98304]{1,0:T(4,128)(2,1)S(1)} reduce(bf16[4,1,98304]{2,0,1:T(4,128)(2,1)} %bitcast.21, bf16[]{:T(256)} %broadcast.17), dimensions={1}, to_apply=%copy.10.reduce_sub_computation | reduce | bytes 1572866 | tf_op jit(solution)/shard_map/all_to_all | solution.py:36
  3.9 0.8 %reshape.33 = bf16[4,2,49152]{2,1,0:T(2,128)(2,1)S(1)} reshape(bf16[4,98304]{1,0:T(4,128)(2,1)S(1)} %reduce.3) | data formatting | bytes 1572864
  4.7 16.3 %all_to_all.9 = bf16[4,2,49152]{2,1,0:T(2,128)(2,1)S(1)} all-to-all(bf16[4,2,49152]{2,1,0:T(2,128)(2,1)S(1)} %reshape.33), channel_id=1, replica_groups=mesh['dp'=4,'shard'=8] {'dp'}, dimensions={0} | all-to-all | bytes 1572864 | tf_op jit(solution)/shard_map/all_to_all | solution.py:36
  21.0 0.7 %reshape.34 = bf16[4,1,98304]{2,1,0:T(2,128)(2,1)S(1)} reshape(bf16[4,2,49152]{2,1,0:T(2,128)(2,1)S(1)} %all_to_all.9) | data formatting | bytes 1572864
  21.8 2.4 %convert_reduce_fusion = f32[98304]{0:T(1024)S(1)} fusion(bf16[4,1,98304]{2,1,0:T(2,128)(2,1)S(1)} %reshape.34), kind=kLoop, calls=%fused_computation | loop fusion | flops 688128 | bytes 1179648 | tf_op jit(solution)/shard_map/reduce_sum | solution.py:37
  24.2 0.0 copy-done
  24.2 0.0 copy-done.3
  24.2 0.0 copy-done.4
  24.2 0.0 copy-start.5
  24.3 0.4 bitcast_reduce_fusion.1
  24.7 0.0 copy-start.1
  24.7 0.0 copy-start.2
  24.7 0.2 copy-done.5
  24.9 0.3 convolution_bitcast_fusion.1
  25.3 0.3 convolution_bitcast_fusion
  25.6 15.1 %all-reduce = (f32[16]{0:T(128)S(1)}, f32[16]{0:T(128)S(1)}) all-reduce(f32[16]{0:T(128)S(1)} %convolution_bitcast_fusion, f32[16]{0:T(128)S(1)} %convolution_bitcast_fusion.1), channel_id=1, replica_groups=mesh['dp'=4,'shard'=8] {'shard'}, use_global_device_ids=true, to_apply=%region_5.0 | all-reduce | flops 32 | bytes 256 | tf_op jit(solution)/shard_map/psum | solution.py:40
  40.7 8.7 %all-reduce.1 = (f32[16]{0:T(128)S(1)}, f32[16]{0:T(128)S(1)}) all-reduce(f32[16]{0:T(128)S(1)} %get-tuple-element.6, f32[16]{0:T(128)S(1)} %get-tuple-element.7), channel_id=1, replica_groups=mesh['dp'=4,'shard'=8] {'dp'}, use_global_device_ids=true, to_apply=%region_6.0 | all-reduce | flops 32 | bytes 256 | tf_op jit(solution)/shard_map/psum | solution.py:39
  49.5 0.4 convolution_reduce_fusion
  49.9 1.0 %fusion.10 = (bf16[98304]{0:T(1024)(128)(2,1)S(1)}, f32[98304]{0:T(1024)}) fusion(f32[98304]{0:T(1024)S(1)} %copy-done, f32[768]{0:T(1024)S(1)} %convolution_reduce_fusion, f32[98304]{0:T(1024)S(1)} %get-tuple-element.13, f32[98304]{0:T(1024)S(1)} %get-tuple-element.12), kind=kLoop, calls=%fused_computation.22 | loop fusion | flops 983040 | bytes 1772544 | tf_op jit(solution)/shard_map/convert_element_type | solution.py:47
  50.9 11.0 %all-gather = bf16[393216]{0:T(1024)(128)(2,1)S(1)} all-gather(bf16[98304]{0:T(1024)(128)(2,1)S(1)} %get-tuple-element.10), channel_id=2, replica_groups=mesh['dp'=4,'shard'=8] {'dp'}, dimensions={0}, use_global_device_ids=true | all-gather | bytes 983040 | tf_op jit(solution)/shard_map/all_gather | solution.py:48
  61.9 0.0 copy-done.1
  61.9 0.0 copy-done.2
  61.9 1.2 %reshape.25 = bf16[4,98304]{1,0:T(4,128)(2,1)} reshape(bf16[393216]{0:T(1024)(128)(2,1)S(1)} %all-gather) | data formatting | bytes 1572864 | tf_op jit(solution)/shard_map/all_gather | solution.py:48
  (5 shorter events, 0.0 us)
Async XLA Ops:
  21.0 3.2 %copy-start = (f32[98304]{0:T(1024)S(1)}, f32[98304]{0:T(1024)}, u32[]{:S(2)}) copy-start(f32[98304]{0:T(1024)} %param.6) | copy-start | bytes 1179652
  21.0 3.2 %copy-start.3 = (f32[98304]{0:T(1024)S(1)}, f32[98304]{0:T(1024)}, u32[]{:S(2)}) copy-start(f32[98304]{0:T(1024)} %param.7) | copy-start | bytes 1179652
  21.0 3.2 %copy-start.4 = (f32[98304]{0:T(1024)S(1)}, f32[98304]{0:T(1024)}, u32[]{:S(2)}) copy-start(f32[98304]{0:T(1024)} %param.8) | copy-start | bytes 1179652
  24.2 0.7 %copy-start.5 = (s32[768]{0:T(1024)S(1)}, s32[768]{0:T(1024)}, u32[]{:S(2)}) copy-start(s32[768]{0:T(1024)} %param.9) | copy-start | bytes 9220
  24.7 37.2 %copy-start.1 = (f32[98304]{0:T(1024)}, f32[98304]{0:T(1024)S(1)}, u32[]{:S(2)}) copy-start(f32[98304]{0:T(1024)S(1)} %get-tuple-element.12) | copy-start | bytes 1179652
  24.7 37.2 %copy-start.2 = (f32[98304]{0:T(1024)}, f32[98304]{0:T(1024)S(1)}, u32[]{:S(2)}) copy-start(f32[98304]{0:T(1024)S(1)} %get-tuple-element.13) | copy-start | bytes 1179652
